TPU v7x, 32 devices: a whole 2x2x4 slice. The times are simulated.
32 devices in a mesh: blk: 8 (over z, y), grp: 4 (over x, core).
Axes of the slice: x: 2, y: 2, z: 4, core: 2. Of those that a mesh axis runs over, the one named last changes fastest.
Arguments:
- embeddings: bfloat16 [4096, 1024], P(('blk', 'grp')), may hold values from -100 to 100
- labels: int32 [4096], P(('blk', 'grp')), may hold values from 0 to 4999, as said below
Outputs:
- anchor_loss: float32 [1024], P(('blk', 'grp'))
- mean_loss: float32 [], replicated
Inputs may be any that keep to these rules, and one draw needn't show every extreme that they name: `labels`: A label of 1000 or more belongs to one sample only.
All inputs are finite; a program needn't handle non-finite values.
Results may differ from a plain program's by a relative error of at most 0.0003.
Values may be sent and summed in bfloat16 or wider, within the bound.
A program may use at most 64 MiB of HBM per device.

v0:
```python
import jax
import jax.numpy as jnp
from jax import lax
from jax.sharding import PartitionSpec as P

A_DEV = 32


def make_fold(anchors, anchor_labels, anchor_ids, key_id_of):

    def fold(carry, pieces, start):
        keys, key_labels = pieces
        where_at = jnp.arange(keys.shape[0], dtype=jnp.int32)
        key_ids = key_id_of(where_at)
        score = (
            lax.dot_general(
                anchors, keys, (((1,), (1,)), ((), ())), preferred_element_type=jnp.float32
            )
            * 10.0
        )
        self_mask = anchor_ids[:, None] == key_ids[None, :]
        expo = jnp.where(self_mask, 0.0, jnp.exp(score - 10.0))
        positive = (anchor_labels[:, None] == key_labels[None, :]) & jnp.logical_not(self_mask)
        return (
            jnp.sum(expo, axis=1),
            jnp.sum(jnp.where(positive, score, 0.0), axis=1),
            jnp.sum(positive.astype(jnp.float32), axis=1),
        )

    return fold


def local(embeddings, labels):
    rows = embeddings.shape[0]
    values = embeddings.astype(jnp.float32)
    unit = (values * lax.rsqrt(jnp.sum(values * values, axis=1, keepdims=True) + 1e-06)).astype(
        jnp.bfloat16
    )
    own_anchors = unit[:A_DEV]
    own_labels = labels[:A_DEV]
    blk_index = lax.axis_index("blk")
    grp_index = lax.axis_index("grp")
    grp_count = lax.axis_size("grp")

    def strided_key(where_at):
        return (where_at // rows * grp_count + grp_index) * rows + where_at % rows

    positions = jnp.arange(A_DEV * grp_count, dtype=jnp.int32)
    anchors, anchor_labels = (
        lax.all_gather(own_anchors, "grp", axis=0, tiled=True),
        lax.all_gather(own_labels, "grp", axis=0, tiled=True),
    )
    anchor_ids = (blk_index * grp_count + positions // A_DEV) * rows + positions % A_DEV
    zeros = jnp.zeros((anchors.shape[0],), jnp.float32)
    fold = make_fold(anchors, anchor_labels, anchor_ids, strided_key)
    totals = fold(
        (zeros, zeros, zeros),
        (
            lax.all_gather(unit, "blk", axis=0, tiled=True),
            lax.all_gather(labels, "blk", axis=0, tiled=True),
        ),
        jnp.int32(0),
    )
    denom, pos_sum, count = (
        lax.psum_scatter(totals[0], "grp", scatter_dimension=0, tiled=True),
        lax.psum_scatter(totals[1], "grp", scatter_dimension=0, tiled=True),
        lax.psum_scatter(totals[2], "grp", scatter_dimension=0, tiled=True),
    )
    valid = count > 0.0
    anchor_loss = jnp.where(valid, jnp.log(denom) + 10.0 - pos_sum / jnp.maximum(count, 1.0), 0.0)
    loss_total, valid_total = lax.psum(
        (jnp.sum(anchor_loss), jnp.sum(valid.astype(jnp.float32))), ("blk", "grp")
    )
    mean_loss = loss_total / jnp.maximum(valid_total, 1.0)
    return (anchor_loss, mean_loss)


def solution(mesh):
    placed = (P(("blk", "grp"), None), P(("blk", "grp")))
    return jax.shard_map(
        local, mesh=mesh, in_specs=placed, out_specs=(P(("blk", "grp")), P()), check_vma=False
    )
```

profile of v0, /device:TPU:0, one launch (start us, length us, event | category | flops | bytes accessed | tf_op | source)
XLA Modules:
  0.0 120.6 jit_solution(12838552396629161836)
XLA Ops:
  7.2 0.0 all-gather.3.cloned.1.call-start
  7.2 1.1 fusion
  8.3 1.8 %fusion.1 = bf16[128,1024]{1,0:T(8,128)(2,1)} fusion(bf16[128,1024]{1,0:T(8,128)(2,1)} %param.2, f32[128]{0:T(128)S(1)} %add_rsqrt_fusion), kind=kLoop, calls=%fused_computation.6 | loop fusion | flops 393216 | bytes 524800 | tf_op jit(solution)/shard_map/convert_element_type | solution.py:36
  10.1 0.0 all-gather.3.cloned.1.call-update
  10.1 0.8 slice.8
  11.0 1.3 %fusion.22 = (u32[1]{0:T(128)}, u32[1]{0:T(128)}) fusion(u32[32]{0:T(128)} %constant.88, u32[]{:T(128)S(6)} %add.107, u32[]{:T(128)S(6)} %add.104), kind=kLoop, calls=%fused_computation.44 | loop fusion | bytes 24
  13.6 0.8 slice_dynamic-update-slice_fusion
  14.4 6.4 %all-reduce = s32[128]{0:T(128)S(1)} all-reduce(s32[128]{0:T(128)S(1)} %slice_dynamic-update-slice_fusion), channel_id=1, replica_groups=mesh['blk'=8,'grp'=4] {'grp'}, use_global_device_ids=true, to_apply=%add | all-reduce | flops 128 | bytes 1024
  20.7 21.0 %all-gather = s32[8,1,128]{2,1,0:T(1,128)S(1)} all-gather(s32[1,1,128]{2,1,0:T(1,128)} %bitcast.7), channel_id=1, replica_groups=mesh['blk'=8,'grp'=4] {'blk'}, dimensions={0}, use_global_device_ids=true | all-gather | bytes 4608 | tf_op jit(solution)/shard_map/all_gather | solution.py:60
  41.7 5.8 %all_gather.14 = bf16[128,1024]{1,0:T(8,128)(2,1)S(1)} all-gather(bf16[32,1024]{1,0:T(8,128)(2,1)S(1)} %slice.8), channel_id=1, replica_groups=mesh['blk'=8,'grp'=4] {'grp'}, dimensions={0}, use_global_device_ids=true | all-gather | bytes 327680 | tf_op jit(solution)/shard_map/all_gather | solution.py:50
  47.5 14.6 %all-gather.3.cloned.1.call-done = bf16[1024,1024]{1,0:T(8,128)(2,1)} async-done(((bf16[128,1024]{1,0:T(8,128)(2,1)}), bf16[1024,1024]{1,0:T(8,128)(2,1)}) %all-gather.3.cloned.1.call-update) | async-done | bytes 2097168 | tf_op jit(solution)/shard_map/all_gather | solution.py:59
  62.1 2.6 %fusion.2 = (f32[128]{0:T(128)S(1)}, f32[128]{0:T(128)S(1)}, f32[128]{0:T(128)S(1)}) fusion(s32[1024]{0:T(1024)S(1)} %fusion.13, s32[128]{0:T(128)S(1)} %fusion.15, s32[1024]{0:T(1024)S(1)} %bitcast.6, s32[128]{0:T(128)S(1)} %all-reduce, bf16[128,1024]{1,0:T(8,128)(2,1)S(1)} %all_gather.14, bf16[1024,1024]{1,0:T(8,128)(2,1)} %all-gather.3.cloned.1.call-done), kind=kOutput, calls=%fused_computation.7 | convolution fusion | flops 270007936 | bytes 2370048 | tf_op jit(solution)/shard_map/dot_general | solution.py:16
  64.8 5.7 %all-reduce.5 = (f32[128]{0:T(128)S(1)}, f32[128]{0:T(128)S(1)}, f32[128]{0:T(128)S(1)}) all-reduce(f32[128]{0:T(128)S(1)} %get-tuple-element.3, f32[128]{0:T(128)S(1)} %get-tuple-element.2, f32[128]{0:T(128)S(1)} %get-tuple-element.4), channel_id=4, replica_groups=mesh['blk'=8,'grp'=4] {'grp'}, use_global_device_ids=true, to_apply=%region_6.7.clone | all-reduce | flops 384 | bytes 3072
  70.4 1.3 %fusion.21 = (f32[]{:T(128)}, f32[32]{0:T(128)}, f32[]{:T(128)}) fusion(f32[128]{0:T(128)S(1)} %get-tuple-element.7, u32[]{:T(128)S(6)} %multiply.4, f32[128]{0:T(128)S(1)} %get-tuple-element.8, f32[128]{0:T(128)S(1)} %get-tuple-element.9), kind=kLoop, calls=%fused_computation.43 | loop fusion | flops 286 | bytes 524 | tf_op jit(solution)/shard_map/reduce_sum | solution.py:72
  71.7 39.7 %all-reduce.4 = (f32[]{:T(128)}, f32[]{:T(128)}) all-reduce(f32[]{:T(128)} %get-tuple-element.10, f32[]{:T(128)} %get-tuple-element.12), channel_id=1, replica_groups=mesh['blk'=8,'grp'=4] {'blk','grp'}, use_global_device_ids=true, to_apply=%region_8.9 | all-reduce | flops 2 | bytes 16 | tf_op jit(solution)/shard_map/psum | solution.py:71
  (4 shorter events, 0.0 us)
Async XLA Ops:
  7.2 54.9 %all-gather.3.cloned.1.call-start = ((), (), s32[]{:S(2)}) async-start(), calls=%async_computation | async-start | bytes 2359296 | tf_op jit(solution)/shard_map/all_gather | solution.py:59
Sparse Core Ops, SparseCore 0:
  10.2 51.8 all-gather.2
where the time goes:
time: 121 us
  blocking collectives  78.5 us (65%)
  between operations  17.7 us (15%)
  waiting for transfers between devices  14.6 us (12%)
  other arithmetic  4.18 us (3%)
  local copies, waits for them, and re-layouts  2.92 us (2%)
  matrix products  2.65 us (2%)
    psum x1, blocking collectives, local(): lax.psum((jnp.sum(anchor_loss), jnp.sum(valid.astype(jnp.float32))), ('bl...  39.7 us
    all_gather x1, blocking collectives, local(): lax.all_gather(labels, 'blk', axis=0, tiled=True)  21 us
    all_gather x1, waiting for transfers between devices, local(): lax.all_gather(unit, 'blk', axis=0, tiled=True)  14.6 us
    unnamed x2, blocking collectives  12 us
    all_gather x1, blocking collectives, local(): lax.all_gather(own_anchors, 'grp', axis=0, tiled=True)  5.76 us
    dot_general x1, matrix products, fold(): lax.dot_general(anchors, keys, (((1,), (1,)), ((), ())), preferred_elemen...  2.65 us
  transfers between devices with their start and end apart: 1, of which 1 were waited for; matrix products, arithmetic and copies ran while one was open for 2% of the time, Pallas kernels for 0%

commit v1 on v0

v1 whole, which is shorter than its diff:
```python
import functools

import jax
import jax.numpy as jnp
from jax import lax
from jax.experimental import pallas as pl
from jax.experimental.pallas import tpu as pltpu
from jax.sharding import PartitionSpec as P

A_DEV = 32
LANES = 128
MESH = pl.DeviceIdType.MESH


def flip(value, bits):
    out, bit = value, 1
    while bit <= bits:
        if bits & bit:
            out = out + bit - 2 * bit * ((value // bit) % 2)
        bit *= 2
    return out


def partner(value, step, count):
    if count & (count - 1) == 0:
        other = flip(value, step)
        return other, other
    return (value + step) % count, (value + count - step) % count


def kernel(
    sizes, emb_hbm, lab_ref, out_ref,
    emb, keys, anc, lab_k, lab_a, part,
    emb_sem, key_send, key_recv, anc_send, anc_recv, lab_send, lab_k_recv, lab_a_recv, part_send, part_recv,
):
    nb, ng, ny, nc, rows, chunks = sizes
    nz, nx = nb // ny, ng // nc
    count = nb * ng
    groups = nb * A_DEV // LANES
    per_group = LANES // A_DEV
    b, g = lax.axis_index("blk"), lax.axis_index("grp")
    z, y = b // ny, b % ny
    x, c = g // nc, g % nc
    me = b * ng + g

    load = pltpu.make_async_copy(emb_hbm, emb, emb_sem)
    load.start()

    barrier = pltpu.get_barrier_semaphore()

    def greet(step, carry):
        t = (me + step) % count
        pl.semaphore_signal(barrier, inc=1, device_id=(t // ng, t % ng), device_id_type=MESH)
        return carry

    lax.fori_loop(1, count, greet, 0)

    lab_row = lab_ref[...]
    lab_tile = jnp.broadcast_to(lab_row, (8, LANES))
    lab_k[g] = lab_tile
    lab_a[b] = lab_tile

    load.wait()
    values = emb[...].astype(jnp.float32)
    unit = (values * lax.rsqrt(jnp.sum(values * values, axis=1, keepdims=True) + 1e-06)).astype(jnp.bfloat16)

    def key_at(block, chunk=None):
        if chunk is None:
            return keys.at[pl.ds(pl.multiple_of(block * rows, rows), rows)]
        size = rows // chunks
        return keys.at[pl.ds(pl.multiple_of(block * rows + chunk * size, size), size)]

    def anc_at(block):
        return anc.at[pl.ds(pl.multiple_of(block * A_DEV, A_DEV), A_DEV)]

    key_at(g)[...] = unit
    anc_at(b)[...] = unit[:A_DEV]
    pl.semaphore_wait(barrier, count - 1)

    sends = []

    def send(src, dst, send_sem, recv_sem, device):
        copy = pltpu.make_async_remote_copy(
            src_ref=src, dst_ref=dst, send_sem=send_sem, recv_sem=recv_sem,
            device_id=device, device_id_type=MESH,
        )
        copy.start()
        sends.append(copy)

    def arrived(ref, sem):
        pltpu.make_async_copy(ref, ref, sem).wait()

    slot = 0
    for step in range(1, nz):
        to, _ = partner(z, step, nz)
        send(anc_at(b), anc_at(b), anc_send.at[slot], anc_recv.at[b], (to * ny + y, g))
        slot += 1
    kslot = 0
    for chunk in range(chunks):
        for step in range(1, nx):
            to, _ = partner(x, step, nx)
            send(key_at(g, chunk), key_at(g, chunk), key_send.at[kslot], key_recv.at[g, chunk], (b, to * nc + c))
            kslot += 1
    for step in range(1, ny):
        send(anc_at(b), anc_at(b), anc_send.at[slot], anc_recv.at[b], (z * ny + partner(y, step, ny)[0], g))
        slot += 1
    for step in range(1, nc):
        for chunk in range(chunks):
            send(key_at(g, chunk), key_at(g, chunk), key_send.at[kslot], key_recv.at[g, chunk],
                 (b, x * nc + partner(c, step, nc)[0]))
            kslot += 1
    lslot = 0
    for step in range(1, nb):
        send(lab_a.at[b], lab_a.at[b], lab_send.at[lslot], lab_a_recv, ((b + step) % nb, g))
        lslot += 1
    for step in range(1, ng):
        send(lab_k.at[g], lab_k.at[g], lab_send.at[lslot], lab_k_recv, (b, (g + step) % ng))
        lslot += 1

    key_jobs = [(step, chunk) for chunk in range(chunks) for step in range(1, nx)]
    anc_jobs = list(range(1, nz))
    for turn in range(max(len(key_jobs), len(anc_jobs))):
        if turn < len(anc_jobs):
            source = partner(z, anc_jobs[turn], nz)[1] * ny + y
            arrived(anc_at(source), anc_recv.at[source])
            for step in range(1, ny):
                send(anc_at(source), anc_at(source), anc_send.at[slot], anc_recv.at[source],
                     (z * ny + partner(y, step, ny)[0], g))
                slot += 1
        if turn < len(key_jobs):
            step, chunk = key_jobs[turn]
            source = partner(x, step, nx)[1] * nc + c
            arrived(key_at(source, chunk), key_recv.at[source, chunk])
            for hop in range(1, nc):
                send(key_at(source, chunk), key_at(source, chunk), key_send.at[kslot], key_recv.at[source, chunk],
                     (b, x * nc + partner(c, hop, nc)[0]))
                kslot += 1
    if nb > 1:
        arrived(lab_a.at[pl.ds(0, nb - 1)], lab_a_recv)
    if ng > 1:
        arrived(lab_k.at[pl.ds(0, ng - 1)], lab_k_recv)
    for hop in range(1, ny):
        for step in range(nz):
            source = (partner(z, step, nz)[1] if step else z) * ny + partner(y, hop, ny)[1]
            arrived(anc_at(source), anc_recv.at[source])
    for hop in range(1, nc):
        for step in range(nx):
            source = (partner(x, step, nx)[1] if step else x) * nc + partner(c, hop, nc)[1]
            for chunk in range(chunks):
                arrived(key_at(source, chunk), key_recv.at[source, chunk])

    lane = lax.broadcasted_iota(jnp.int32, (8, LANES), 1)
    lane_full = lax.broadcasted_iota(jnp.int32, (rows, LANES), 1)
    row_full = lax.broadcasted_iota(jnp.int32, (rows, LANES), 0)
    anchor_labels = []
    for h in range(groups):
        tile = lab_a[h * per_group]
        for q in range(1, per_group):
            tile = jnp.where(lane // A_DEV == q, pltpu.roll(lab_a[h * per_group + q], q * A_DEV, 1), tile)
        anchor_labels.append(tile[:1])

    def fold(block, carry):
        at = pl.ds(pl.multiple_of(block * rows, rows), rows)
        score = lax.dot_general(
            keys[at], anc[...], (((1,), (1,)), ((), ())), preferred_element_type=jnp.float32
        ) * 10.0
        key_labels = jnp.transpose(jnp.broadcast_to(lab_k[block][:1], (LANES, LANES)))
        key_ids = (b * ng + block) * rows + row_full
        out = []
        for h in range(groups):
            part_score = score[:, h * LANES:(h + 1) * LANES]
            anchor_block = h * per_group + lane_full // A_DEV
            anchor_ids = (anchor_block * ng + g) * rows + lane_full % A_DEV
            self_mask = anchor_ids == key_ids
            expo = jnp.where(self_mask, 0.0, jnp.exp(part_score - 10.0))
            positive = (key_labels == anchor_labels[h]) & jnp.logical_not(self_mask)
            out += [
                carry[3 * h] + jnp.sum(expo, axis=0, keepdims=True),
                carry[3 * h + 1] + jnp.sum(jnp.where(positive, part_score, 0.0), axis=0, keepdims=True),
                carry[3 * h + 2] + jnp.sum(jnp.where(positive, 1.0, 0.0), axis=0, keepdims=True),
            ]
        return tuple(out)

    zero = jnp.zeros((1, LANES), jnp.float32)
    totals = lax.fori_loop(0, ng, fold, (zero,) * (3 * groups), unroll=ng <= 4)
    tall = part.shape[1]
    pad = [jnp.zeros((tall - 3 * groups, LANES), jnp.float32)] if tall > 3 * groups else []
    part[me] = jnp.concatenate(list(totals) + pad, axis=0)

    def tell(step, carry):
        t = (me + step) % count
        pltpu.make_async_remote_copy(
            src_ref=part.at[me], dst_ref=part.at[me], send_sem=part_send, recv_sem=part_recv,
            device_id=(t // ng, t % ng), device_id_type=MESH,
        ).start()
        return carry

    lax.fori_loop(1, count, tell, 0)
    for copy in sends:
        copy.wait_send()
    arrived(part.at[pl.ds(0, count - 1)], part_recv)

    every = jnp.sum(part[...].reshape(nb, ng, tall, LANES), axis=0)
    loss_total, valid_total, own = zero, zero, zero
    for other in range(ng):
        for h in range(groups):
            denom = every[other, 3 * h:3 * h + 1]
            pos_sum = every[other, 3 * h + 1:3 * h + 2]
            number = every[other, 3 * h + 2:3 * h + 3]
            valid = number > 0.0
            loss = jnp.where(valid, jnp.log(denom) + 10.0 - pos_sum / jnp.maximum(number, 1.0), 0.0)
            loss_total += loss
            valid_total += jnp.where(valid, 1.0, 0.0)
            own = jnp.where(g * groups + b // per_group == other * groups + h, loss, own)
    total = jnp.sum(loss_total, axis=1, keepdims=True)
    valid_sum = jnp.sum(valid_total, axis=1, keepdims=True)
    mean = total / jnp.maximum(valid_sum, 1.0)
    shift = (LANES - (b % per_group) * A_DEV) % LANES
    own = pltpu.roll(jnp.broadcast_to(own, (8, LANES)), shift, 1)
    sub = lax.broadcasted_iota(jnp.int32, (8, LANES), 0)
    out_ref[...] = jnp.where(sub == 0, own, jnp.broadcast_to(mean, (8, LANES)))
    arrived(part.at[pl.ds(0, count - 1)], part_send)


def solution(mesh):
    nb, ng = mesh.shape["blk"], mesh.shape["grp"]
    ny = 2 if nb % 2 == 0 else 1
    nc = 2 if ng % 2 == 0 else 1

    def local(embeddings, labels):
        rows, width = embeddings.shape
        chunks = 4
        groups = nb * A_DEV // LANES
        tall = -(-3 * groups // 8) * 8
        sizes = (nb, ng, ny, nc, rows, chunks)
        dma = pltpu.SemaphoreType.DMA
        out = pl.pallas_call(
            functools.partial(kernel, sizes),
            name="contrast",
            out_shape=jax.ShapeDtypeStruct((8, LANES), jnp.float32),
            in_specs=[pl.BlockSpec(memory_space=pl.ANY), pl.BlockSpec(memory_space=pltpu.VMEM)],
            out_specs=pl.BlockSpec(memory_space=pltpu.VMEM),
            scratch_shapes=[
                pltpu.VMEM((rows, width), jnp.bfloat16),
                pltpu.VMEM((ng * rows, width), jnp.bfloat16),
                pltpu.VMEM((nb * A_DEV, width), jnp.bfloat16),
                pltpu.VMEM((ng, 8, LANES), jnp.int32),
                pltpu.VMEM((nb, 8, LANES), jnp.int32),
                pltpu.VMEM((nb * ng, tall, LANES), jnp.float32),
                dma,
                dma((ng * chunks,)),
                dma((ng, chunks)),
                dma((nb,)),
                dma((nb,)),
                dma((nb + ng,)),
                dma,
                dma,
                dma,
                dma,
            ],
            compiler_params=pltpu.CompilerParams(
                collective_id=0, has_side_effects=True, vmem_limit_bytes=48 * 1024 * 1024
            ),
        )(embeddings, labels.reshape(1, rows))
        return out[0, :A_DEV], out[1, 0]

    placed = (P(("blk", "grp"), None), P(("blk", "grp")))
    return jax.shard_map(
        local, mesh=mesh, in_specs=placed, out_specs=(P(("blk", "grp")), P()), check_vma=False
    )
```

time: 121 us -> 27.3 us (0.23)
  blocking collectives: 78.5 us -> 0 us
  Pallas kernels: 0 us -> 23.9 us
  between operations: 17.7 us -> 0.65 us
  waiting for transfers between devices: 14.6 us -> 0 us
  other arithmetic: 4.18 us -> 0 us
  matrix products: 2.65 us -> 0 us
    psum x1 -> x0, blocking collectives: 39.7 us -> none  [local(): lax.psum((jnp.sum(anchor_loss), jnp.sum(valid.astype(jnp.float32))), ('bl...]
    all_gather x2 -> x0, blocking collectives: 26.8 us -> none  [the longest x1 21 us: local(): lax.all_gather(labels, 'blk', axis=0, tiled=True)]
    pallas_call x0 -> x1, Pallas kernels: none -> 23.9 us  [local(): pl.pallas_call(functools.partial(kernel, sizes), name='contrast', out_sha...]
    all_gather x1 -> x0, waiting for transfers between devices: 14.6 us -> none  [local(): lax.all_gather(unit, 'blk', axis=0, tiled=True)]
    unnamed x2 -> x0, blocking collectives: 12 us -> none
    dot_general x1 -> x0, matrix products: 2.65 us -> none  [fold(): lax.dot_general(anchors, keys, (((1,), (1,)), ((), ())), preferred_elemen...]
    reduce_sum x2 -> x0, other arithmetic: 2.36 us -> none  [the longest x1 1.28 us: local(): jnp.sum(anchor_loss)]
    convert_element_type x1 -> x0, other arithmetic: 1.79 us -> none  [local(): (values * lax.rsqrt(jnp.sum(values * values, axis=1, keepdims=True) + 1e-...]
  transfers between devices with their start and end apart: 1 -> 0, of which waited for: 1 -> 0; matrix products, arithmetic and copies ran while one was open for 2% -> 0% of each run, Pallas kernels for 0% -> 0%
where the time goes in v1:
time: 27.3 us; the launch traced here: 27.2 us
  Pallas kernels  23.9 us (88%)
  local copies, waits for them, and re-layouts  2.62 us (10%)
  between operations  0.65 us (2%)
    pallas_call x1, Pallas kernels, local(): pl.pallas_call(functools.partial(kernel, sizes), name='contrast', out_sha...  23.9 us
    unnamed x4, local copies, waits for them, and re-layouts  1.6 us

profile of v1, /device:TPU:0, one launch (start us, length us, event | category | flops | bytes accessed | tf_op | source)
XLA Modules:
  0.0 27.2 jit_solution(10760948465447898731)
XLA Ops:
  0.6 0.0 copy-start.1
  0.6 0.6 %copy-done.1 = s32[128]{0:T(128)S(1)} copy-done((s32[128]{0:T(128)S(1)}, s32[128]{0:T(128)}, u32[]{:S(2)}) %copy-start.1) | copy-done | bytes 536
  1.3 0.0 copy-start
  1.3 0.9 %copy-done = bf16[128,1024]{1,0:T(8,128)(2,1)S(1)} copy-done((bf16[128,1024]{1,0:T(8,128)(2,1)S(1)}, bf16[128,1024]{1,0:T(8,128)(2,1)}, u32[]{:S(2)}) %copy-start) | copy-done | bytes 262168
  2.2 23.9 %contrast.1 = f32[8,128]{1,0:T(8,128)S(1)} custom-call(bf16[128,1024]{1,0:T(8,128)(2,1)S(1)} %copy-done, s32[1,128]{1,0:T(1,128)S(1)} %bitcast.4), custom_call_target="tpu_custom_call" | custom-call | tf_op jit(solution)/shard_map/contrast/pallas_call | solution.py:237
  26.1 0.5 %slice.7 = f32[1,1]{1,0:T(1,128)} slice(f32[8,128]{1,0:T(8,128)S(1)} %contrast.1), slice={[1:2], [0:1]} | slice | bytes 8 | tf_op jit(solution)/shard_map/slice | solution.py:265
  26.7 0.5 %slice_bitcast_fusion = f32[32]{0:T(128)} fusion(f32[8,128]{1,0:T(8,128)S(1)} %contrast.1), kind=kLoop, calls=%fused_computation | loop fusion | bytes 256 | tf_op jit(solution)/shard_map/squeeze | solution.py:265
Async XLA Ops:
  0.6 0.7 %copy-start.1 = (s32[128]{0:T(128)S(1)}, s32[128]{0:T(128)}, u32[]{:S(2)}) copy-start(s32[128]{0:T(128)} %param.3) | copy-start | bytes 1540
  1.3 0.9 %copy-start = (bf16[128,1024]{1,0:T(8,128)(2,1)S(1)}, bf16[128,1024]{1,0:T(8,128)(2,1)}, u32[]{:S(2)}) copy-start(bf16[128,1024]{1,0:T(8,128)(2,1)} %emb_hbm.1) | copy-start | bytes 786436

commit v2 on v1

v2 whole, which is shorter than its diff:
```python
import functools

import jax
import jax.numpy as jnp
from jax import lax
from jax.experimental import pallas as pl
from jax.experimental.pallas import tpu as pltpu
from jax.sharding import PartitionSpec as P

A_DEV = 32
LANES = 128
MESH = pl.DeviceIdType.MESH


def flip(value, bits):
    out, bit = value, 1
    while bit <= bits:
        if bits & bit:
            out = out + bit - 2 * bit * ((value // bit) % 2)
        bit *= 2
    return out


def partner(value, step, count):
    if count & (count - 1) == 0:
        other = flip(value, step)
        return other, other
    return (value + step) % count, (value + count - step) % count


def kernel(
    sizes, emb_hbm, lab_hbm, out_ref,
    emb, lab_ref, keys, anc, lab_k, lab_a, lab_col, part,
    emb_sem, lab_sem, key_send, key_recv, anc_send, anc_recv, lab_send, lab_k_recv, lab_a_recv, part_send, part_recv,
):
    nb, ng, ny, nc, rows, chunks, cuts = sizes
    nz, nx = nb // ny, ng // nc
    count = nb * ng
    groups = nb * A_DEV // LANES
    per_group = LANES // A_DEV
    b, g = lax.axis_index("blk"), lax.axis_index("grp")
    z, y = b // ny, b % ny
    x, c = g // nc, g % nc
    me = b * ng + g

    load = pltpu.make_async_copy(emb_hbm, emb, emb_sem)
    load.start()
    load_labels = pltpu.make_async_copy(lab_hbm, lab_ref, lab_sem)
    load_labels.start()

    barrier = pltpu.get_barrier_semaphore()

    for step in range(1, nb):
        pl.semaphore_signal(barrier, inc=1, device_id=((b + step) % nb, g), device_id_type=MESH)
    for step in range(1, ng):
        pl.semaphore_signal(barrier, inc=1, device_id=(b, (g + step) % ng), device_id_type=MESH)

    load_labels.wait()
    lab_row = lab_ref[...]
    lab_k[g] = lab_row
    lab_a[b] = lab_row

    load.wait()
    values = emb[...].astype(jnp.float32)
    unit = (values * lax.rsqrt(jnp.sum(values * values, axis=1, keepdims=True) + 1e-06)).astype(jnp.bfloat16)

    def key_at(block, chunk=None):
        if chunk is None:
            return keys.at[pl.ds(pl.multiple_of(block * rows, rows), rows)]
        size = rows // chunks
        return keys.at[pl.ds(pl.multiple_of(block * rows + chunk * size, size), size)]

    piece = A_DEV // cuts

    def anc_at(block, cut=None):
        if cut is None:
            return anc.at[pl.ds(pl.multiple_of(block * A_DEV, A_DEV), A_DEV)]
        return anc.at[pl.ds(pl.multiple_of(block * A_DEV + cut * piece, piece), piece)]

    key_at(g)[...] = unit
    anc_at(b)[...] = unit[:A_DEV]
    pl.semaphore_wait(barrier, nb + ng - 2)

    sends = []

    def send(src, dst, send_sem, recv_sem, device):
        copy = pltpu.make_async_remote_copy(
            src_ref=src, dst_ref=dst, send_sem=send_sem, recv_sem=recv_sem,
            device_id=device, device_id_type=MESH,
        )
        copy.start()
        sends.append(copy)

    def arrived(ref, sem):
        pltpu.make_async_copy(ref, ref, sem).wait()

    lslot = 0
    for step in range(1, nb):
        send(lab_a.at[b], lab_a.at[b], lab_send.at[lslot], lab_a_recv, ((b + step) % nb, g))
        lslot += 1
    for step in range(1, ng):
        send(lab_k.at[g], lab_k.at[g], lab_send.at[lslot], lab_k_recv, (b, (g + step) % ng))
        lslot += 1
    slot, kslot = 0, 0

    def send_anchors(block, cut, device):
        nonlocal slot
        send(anc_at(block, cut), anc_at(block, cut), anc_send.at[slot], anc_recv.at[block, cut], device)
        slot += 1

    def send_keys(block, chunk, device):
        nonlocal kslot
        send(key_at(block, chunk), key_at(block, chunk), key_send.at[kslot], key_recv.at[block, chunk], device)
        kslot += 1

    for chunk in range(chunks):
        for step in range(1, nx):
            send_keys(g, chunk, (b, partner(x, step, nx)[0] * nc + c))
    for step in range(1, nz):
        for cut in range(cuts):
            send_anchors(b, cut, (partner(z, step, nz)[0] * ny + y, g))
    for cut in range(cuts):
        for step in range(1, ny):
            send_anchors(b, cut, (z * ny + partner(y, step, ny)[0], g))
    for step in range(1, nc):
        for chunk in range(chunks):
            send_keys(g, chunk, (b, x * nc + partner(c, step, nc)[0]))

    key_jobs = [(step, chunk) for chunk in range(chunks) for step in range(1, nx)]
    anc_jobs = [(step, cut) for step in range(1, nz) for cut in range(cuts)]
    jobs = [((at + 1) / len(key_jobs), 0, job) for at, job in enumerate(key_jobs)]
    jobs += [((at + 1) / len(anc_jobs), 1, job) for at, job in enumerate(anc_jobs)]
    for _, kind, (step, number) in sorted(jobs):
        if kind:
            source = partner(z, step, nz)[1] * ny + y
            arrived(anc_at(source, number), anc_recv.at[source, number])
            for hop in range(1, ny):
                send_anchors(source, number, (z * ny + partner(y, hop, ny)[0], g))
        else:
            source = partner(x, step, nx)[1] * nc + c
            arrived(key_at(source, number), key_recv.at[source, number])
            for hop in range(1, nc):
                send_keys(source, number, (b, x * nc + partner(c, hop, nc)[0]))

    if nb > 1:
        arrived(lab_a.at[pl.ds(0, nb - 1)], lab_a_recv)
    if ng > 1:
        arrived(lab_k.at[pl.ds(0, ng - 1)], lab_k_recv)
    for block in range(ng):
        lab_col[block] = jnp.transpose(jnp.broadcast_to(lab_k[block], (LANES, LANES)))

    lane = lax.broadcasted_iota(jnp.int32, (8, LANES), 1)
    lane_full = lax.broadcasted_iota(jnp.int32, (rows, LANES), 1)
    row_full = lax.broadcasted_iota(jnp.int32, (rows, LANES), 0)

    for hop in range(1, nc):
        for step in range(nx):
            source = (partner(x, step, nx)[1] if step else x) * nc + partner(c, hop, nc)[1]
            for chunk in range(chunks):
                arrived(key_at(source, chunk), key_recv.at[source, chunk])

    zero = jnp.zeros((1, LANES), jnp.float32)

    def fold_group(h):
        tile = jnp.broadcast_to(lab_a[h * per_group], (8, LANES))
        for q in range(1, per_group):
            turned = pltpu.roll(jnp.broadcast_to(lab_a[h * per_group + q], (8, LANES)), q * A_DEV, 1)
            tile = jnp.where(lane // A_DEV == q, turned, tile)
        labels_here = tile[:1]
        anchors = anc[pl.ds(pl.multiple_of(h * LANES, LANES), LANES)]
        anchor_ids = ((h * per_group + lane_full // A_DEV) * ng + g) * rows + lane_full % A_DEV

        def fold(block, carry):
            at = pl.ds(pl.multiple_of(block * rows, rows), rows)
            score = lax.dot_general(
                keys[at], anchors, (((1,), (1,)), ((), ())), preferred_element_type=jnp.float32
            ) * 10.0
            self_mask = anchor_ids == (b * ng + block) * rows + row_full
            expo = jnp.where(self_mask, 0.0, jnp.exp(score - 10.0))
            positive = (lab_col[block] == labels_here) & jnp.logical_not(self_mask)
            return (
                carry[0] + jnp.sum(expo, axis=0, keepdims=True),
                carry[1] + jnp.sum(jnp.where(positive, score, 0.0), axis=0, keepdims=True),
                carry[2] + jnp.sum(jnp.where(positive, 1.0, 0.0), axis=0, keepdims=True),
            )

        return jnp.concatenate(lax.fori_loop(0, ng, fold, (zero,) * 3, unroll=ng <= 4), axis=0)

    near, per_z = b // per_group, max(per_group // ny, 1)
    in_step = nz & (nz - 1) == 0 and groups & (groups - 1) == 0 and per_group % ny == 0
    found = []
    for turn in range(groups):
        first = turn * per_z if in_step else (0 if turn == 0 else nz)
        last = first + per_z if in_step else nz
        for step in range(first, last):
            for hop in range(1, ny):
                source = (partner(z, step, nz)[1] if step else z) * ny + partner(y, hop, ny)[1]
                for cut in range(cuts):
                    arrived(anc_at(source, cut), anc_recv.at[source, cut])
        h = partner(near, turn, groups)[0] if turn else near
        found.append((h, fold_group(h)))
    for h in range(groups):
        mine = found[0][1]
        for other, sums in found[1:]:
            mine = jnp.where(other == h, sums, mine)
        part[me, 3 * h:3 * h + 3] = mine

    def tell(step, carry):
        t = (me + step) % count
        pltpu.make_async_remote_copy(
            src_ref=part.at[me], dst_ref=part.at[me], send_sem=part_send, recv_sem=part_recv,
            device_id=(t // ng, t % ng), device_id_type=MESH,
        ).start()
        return carry

    lax.fori_loop(1, count, tell, 0, unroll=count <= 32)
    for copy in sends:
        copy.wait_send()
    arrived(part.at[pl.ds(0, count - 1)], part_recv)

    tall = part.shape[1]
    every = jnp.sum(part[...].reshape(nb, ng, tall, LANES), axis=0)
    loss_total, valid_total, own = zero, zero, zero
    for other in range(ng):
        for h in range(groups):
            denom = every[other, 3 * h:3 * h + 1]
            pos_sum = every[other, 3 * h + 1:3 * h + 2]
            number = every[other, 3 * h + 2:3 * h + 3]
            valid = number > 0.0
            loss = jnp.where(valid, jnp.log(denom) + 10.0 - pos_sum / jnp.maximum(number, 1.0), 0.0)
            loss_total += loss
            valid_total += jnp.where(valid, 1.0, 0.0)
            own = jnp.where(g * groups + b // per_group == other * groups + h, loss, own)
    total = jnp.sum(loss_total, axis=1, keepdims=True)
    valid_sum = jnp.sum(valid_total, axis=1, keepdims=True)
    mean = total / jnp.maximum(valid_sum, 1.0)
    shift = (LANES - (b % per_group) * A_DEV) % LANES
    own = pltpu.roll(jnp.broadcast_to(own, (8, LANES)), shift, 1)
    sub = lax.broadcasted_iota(jnp.int32, (8, LANES), 0)
    out_ref[...] = jnp.where(sub == 0, own, jnp.broadcast_to(mean, (8, LANES)))
    arrived(part.at[pl.ds(0, count - 1)], part_send)


def solution(mesh):
    nb, ng = mesh.shape["blk"], mesh.shape["grp"]
    ny = 2 if nb % 2 == 0 else 1
    nc = 2 if ng % 2 == 0 else 1

    def local(embeddings, labels):
        rows, width = embeddings.shape
        chunks, cuts = 4, 2
        groups = nb * A_DEV // LANES
        tall = 3 * groups
        sizes = (nb, ng, ny, nc, rows, chunks, cuts)
        dma = pltpu.SemaphoreType.DMA
        out = pl.pallas_call(
            functools.partial(kernel, sizes),
            name="contrast",
            out_shape=jax.ShapeDtypeStruct((8, LANES), jnp.float32),
            in_specs=[pl.BlockSpec(memory_space=pl.ANY)] * 2,
            out_specs=pl.BlockSpec(memory_space=pltpu.VMEM),
            scratch_shapes=[
                pltpu.VMEM((rows, width), jnp.bfloat16),
                pltpu.VMEM((1, rows), jnp.int32),
                pltpu.VMEM((ng * rows, width), jnp.bfloat16),
                pltpu.VMEM((nb * A_DEV, width), jnp.bfloat16),
                pltpu.VMEM((ng, 1, LANES), jnp.int32),
                pltpu.VMEM((nb, 1, LANES), jnp.int32),
                pltpu.VMEM((ng, rows, LANES), jnp.int32),
                pltpu.VMEM((nb * ng, tall, LANES), jnp.float32),
                dma,
                dma,
                dma((ng * chunks,)),
                dma((ng, chunks)),
                dma((nb * cuts,)),
                dma((nb, cuts)),
                dma((nb + ng,)),
                dma,
                dma,
                dma,
                dma,
            ],
            compiler_params=pltpu.CompilerParams(
                collective_id=0, has_side_effects=True
            ),
        )(embeddings, labels.reshape(1, rows))
        return out[0, :A_DEV], out[1, 0]

    placed = (P(("blk", "grp"), None), P(("blk", "grp")))
    return jax.shard_map(
        local, mesh=mesh, in_specs=placed, out_specs=(P(("blk", "grp")), P()), check_vma=False
    )
```

time: 27.3 us -> 25.7 us (0.941)
  Pallas kernels: 23.9 us -> 22.4 us
    unnamed x4 -> x0, local copies, waits for them, and re-layouts: 1.6 us -> none
    pallas_call x1, Pallas kernels: 23.9 us -> 22.4 us  [local(): pl.pallas_call(functools.partial(kernel, sizes), name='contrast', out_sha...]
    slice x1, local copies, waits for them, and re-layouts: 0.51 us -> 1.2 us  [local(): return (out[0, :A_DEV], out[1, 0])]
    squeeze x1, local copies, waits for them, and re-layouts: 0.51 us -> 1.19 us  [local(): return (out[0, :A_DEV], out[1, 0])]
where the time goes in v2:
time: 25.7 us; the launch traced here: 25.5 us
  Pallas kernels  22.4 us (87%)
  local copies, waits for them, and re-layouts  2.39 us (9%)
  between operations  0.64 us (2%)
    pallas_call x1, Pallas kernels, local(): pl.pallas_call(functools.partial(kernel, sizes), name='contrast', out_sha...  22.4 us
    slice x1, local copies, waits for them, and re-layouts, local(): return (out[0, :A_DEV], out[1, 0])  1.2 us
    squeeze x1, local copies, waits for them, and re-layouts, local(): return (out[0, :A_DEV], out[1, 0])  1.19 us

profile of v2, /device:TPU:0, one launch (start us, length us, event | category | flops | bytes accessed | tf_op | source)
XLA Modules:
  0.0 25.5 jit_solution(5770315724014986005)
XLA Ops:
  0.6 22.4 %contrast.1 = f32[8,128]{1,0:T(8,128)} custom-call(bf16[128,1024]{1,0:T(8,128)(2,1)} %emb_hbm.1, s32[1,128]{1,0:T(1,128)} %bitcast.4), custom_call_target="tpu_custom_call" | custom-call | tf_op jit(solution)/shard_map/contrast/pallas_call | solution.py:256
  23.1 1.2 %slice.7 = f32[1,1]{1,0:T(1,128)} slice(f32[8,128]{1,0:T(8,128)} %contrast.1), slice={[1:2], [0:1]} | slice | bytes 8 | tf_op jit(solution)/shard_map/slice | solution.py:287
  24.3 1.2 %slice_bitcast_fusion = f32[32]{0:T(128)} fusion(f32[8,128]{1,0:T(8,128)} %contrast.1), kind=kLoop, calls=%fused_computation | loop fusion | bytes 256 | tf_op jit(solution)/shard_map/squeeze | solution.py:287

commit v3 on v2

--- a/solution.py
+++ b/solution.py
@@ -257,7 +257,7 @@
             functools.partial(kernel, sizes),
             name="contrast",
             out_shape=jax.ShapeDtypeStruct((8, LANES), jnp.float32),
-            in_specs=[pl.BlockSpec(memory_space=pl.ANY)] * 2,
+            in_specs=[pl.BlockSpec(memory_space=pltpu.HBM)] * 2,
             out_specs=pl.BlockSpec(memory_space=pltpu.VMEM),
             scratch_shapes=[
                 pltpu.VMEM((rows, width), jnp.bfloat16),
@@ -281,9 +281,9 @@
                 dma,
             ],
             compiler_params=pltpu.CompilerParams(
-                collective_id=0, has_side_effects=True
+                collective_id=0, has_side_effects=True, vmem_limit_bytes=48 * 1024 * 1024
             ),
-        )(embeddings, labels.reshape(1, rows))
+        )(pltpu.with_memory_space_constraint(embeddings, pltpu.HBM), pltpu.with_memory_space_constraint(labels.reshape(1, rows), pltpu.HBM))
         return out[0, :A_DEV], out[1, 0]
 
     placed = (P(("blk", "grp"), None), P(("blk", "grp")))

time: 25.7 us -> 23.7 us (0.922)
  local copies, waits for them, and re-layouts: 2.39 us -> 1.02 us
  Pallas kernels: 22.4 us -> 21.8 us
    slice x1, local copies, waits for them, and re-layouts: 1.2 us -> 0.51 us  [local(): return (out[0, :A_DEV], out[1, 0])]
    squeeze x1, local copies, waits for them, and re-layouts: 1.19 us -> 0.51 us  [local(): return (out[0, :A_DEV], out[1, 0])]
    pallas_call x1, Pallas kernels: 22.4 us -> 21.8 us  [local(): pl.pallas_call(functools.partial(kernel, sizes), name='contrast', out_sha...]
where the time goes in v3:
time: 23.7 us; the launch traced here: 23.5 us
  Pallas kernels  21.8 us (92%)
  local copies, waits for them, and re-layouts  1.02 us (4%)
  between operations  0.64 us (3%)
    pallas_call x1, Pallas kernels, local(): pl.pallas_call(functools.partial(kernel, sizes), name='contrast', out_sha...  21.8 us
    slice x1, local copies, waits for them, and re-layouts, local(): return (out[0, :A_DEV], out[1, 0])  0.51 us
    squeeze x1, local copies, waits for them, and re-layouts, local(): return (out[0, :A_DEV], out[1, 0])  0.51 us

profile of v3, /device:TPU:0, one launch (start us, length us, event | category | flops | bytes accessed | tf_op | source)
XLA Modules:
  0.0 23.5 jit_solution(14277399977589536658)
XLA Ops:
  0.6 21.8 %contrast.1 = f32[8,128]{1,0:T(8,128)S(1)} custom-call(bf16[128,1024]{1,0:T(8,128)(2,1)} %emb_hbm.1, s32[1,128]{1,0:T(1,128)} %bitcast.4), custom_call_target="tpu_custom_call" | custom-call | tf_op jit(solution)/shard_map/contrast/pallas_call | solution.py:256
  22.5 0.5 %slice.7 = f32[1,1]{1,0:T(1,128)} slice(f32[8,128]{1,0:T(8,128)S(1)} %contrast.1), slice={[1:2], [0:1]} | slice | bytes 8 | tf_op jit(solution)/shard_map/slice | solution.py:287
  23.0 0.5 %slice_bitcast_fusion = f32[32]{0:T(128)} fusion(f32[8,128]{1,0:T(8,128)S(1)} %contrast.1), kind=kLoop, calls=%fused_computation | loop fusion | bytes 256 | tf_op jit(solution)/shard_map/squeeze | solution.py:287
